TPU v7x, 32 devices: a whole 2x2x4 slice. The times are simulated.
32 devices in a mesh: gx: 2 (over x), gy: 4 (over z), gz: 4 (over y, core).
Axes of the slice: x: 2, y: 2, z: 4, core: 2. Of those that a mesh axis runs over, the one named last changes fastest.
Arguments:
- populations: float32 [39, 16, 96, 512], P(None, 'gx', 'gy', 'gz'), may hold values from 0.5 to 1.5
- relax: float32 [16, 96, 512], P('gx', 'gy', 'gz'), may hold values from 0.6 to 1.9
Outputs:
- advanced: float32 [39, 16, 96, 512], P(None, 'gx', 'gy', 'gz')
All inputs are finite; a program needn't handle non-finite values.
Results may differ from a plain program's by a relative error of at most 0.0001.
Values sent between devices are 32-bit elements; how exact they have to be, the bound alone decides.
A program may use at most 128 MiB of HBM per device.

v0:
```python
import jax
import jax.numpy as jnp
from jax import lax
from jax.sharding import PartitionSpec as P


def from_behind(block, axis, distance):
    devices = range(lax.axis_size(axis))
    route = [((i - distance) % len(devices), i) for i in devices]
    return lax.ppermute(block, axis, route)


def lattice():
    speeds = [(0, 0, 0)]
    weights = [1.0 / 12.0]
    for axis in range(3):
        for sign in (1, -1):
            vector = [0, 0, 0]
            vector[axis] = sign
            speeds.append(tuple(vector))
            weights.append(1.0 / 12.0)
    for first in (1, -1):
        for second in (1, -1):
            for third in (1, -1):
                speeds.append((first, second, third))
                weights.append(1.0 / 27.0)
    for axis in range(3):
        for sign in (2, -2):
            vector = [0, 0, 0]
            vector[axis] = sign
            speeds.append(tuple(vector))
            weights.append(2.0 / 135.0)
    for couple in ((0, 1), (0, 2), (1, 2)):
        for first in (2, -2):
            for second in (2, -2):
                vector = [0, 0, 0]
                vector[couple[0]] = first
                vector[couple[1]] = second
                speeds.append(tuple(vector))
                weights.append(1.0 / 432.0)
    for axis in range(3):
        for sign in (3, -3):
            vector = [0, 0, 0]
            vector[axis] = sign
            speeds.append(tuple(vector))
            weights.append(1.0 / 1620.0)
    return (speeds, weights)


def collide(popul, rate):
    speeds, weights = lattice()
    acoustic_wave_rate = 2.0 / 3.0
    inverse = 1.0 / acoustic_wave_rate**0.5
    zeroth_moment_rho = sum((weights[member] * popul[member] for member in range(39)))
    flux = [
        sum(
            (
                weights[member] * speeds[member][axis] * popul[member]
                for member in range(39)
                if speeds[member][axis] != 0
            )
        )
        for axis in range(3)
    ]
    thermal_heat_content = sum(
        (
            weights[member]
            * float(sum((value * value for value in speeds[member])))
            * popul[member]
            for member in range(1, 39)
        )
    )
    velocity = [part / zeroth_moment_rho for part in flux]
    flow_norm_square = (
        velocity[0] * velocity[0] + velocity[1] * velocity[1] + velocity[2] * velocity[2]
    )
    site_kinetic_heat = (thermal_heat_content / zeroth_moment_rho - flow_norm_square) / (
        3.0 * acoustic_wave_rate
    )
    scaled = [part * inverse for part in velocity]
    scaled_square = flow_norm_square / acoustic_wave_rate
    excess_quantity = site_kinetic_heat - 1.0
    results = []
    for member in range(39):
        vector = speeds[member]
        aligned = (
            sum((vector[axis] * inverse * scaled[axis] for axis in range(3) if vector[axis] != 0))
            if member > 0
            else jnp.zeros_like(zeroth_moment_rho)
        )
        speed_square = float(sum((value * value for value in vector))) / acoustic_wave_rate
        aligned_square = aligned * aligned
        hermite = (
            1.0
            + aligned
            + 0.5 * (aligned_square - scaled_square + excess_quantity * (speed_square - 3.0))
            + aligned
            * (aligned_square - 3.0 * scaled_square + 3.0 * excess_quantity * (speed_square - 5.0))
            / 6.0
            + (
                aligned_square * aligned_square
                - 6.0 * aligned_square * scaled_square
                + 3.0 * scaled_square * scaled_square
                + 6.0
                * excess_quantity
                * (aligned_square * (speed_square - 7.0) + scaled_square * (5.0 - speed_square))
                + 3.0
                * excess_quantity
                * excess_quantity
                * (speed_square * speed_square - 10.0 * speed_square + 15.0)
            )
            / 24.0
        )
        maxwellian_target = zeroth_moment_rho * hermite
        results.append(popul[member] - rate * (popul[member] - maxwellian_target))
    return jnp.stack(results)


def propagate(extended, depth):
    speeds, weights = lattice()
    lengths = [extended.shape[dim] - 2 * depth for dim in (1, 2, 3)]
    results = []
    for member in range(39):
        vector = speeds[member]
        starts = [depth - vector[axis] for axis in range(3)]
        results.append(
            extended[
                member,
                starts[0] : starts[0] + lengths[0],
                starts[1] : starts[1] + lengths[1],
                starts[2] : starts[2] + lengths[2],
            ]
        )
    return jnp.stack(results)


def outbound(full, dim, sign):
    speeds, weights = lattice()
    count = full.shape[dim]
    slabs = []
    for member in range(39):
        speed = speeds[member][dim - 1] * sign
        if speed > 0:
            field = full[member]
            if sign > 0:
                layers = lax.slice_in_dim(field, count - speed, count, axis=dim - 1)
            else:
                layers = lax.slice_in_dim(field, 0, speed, axis=dim - 1)
            slabs.append(jnp.moveaxis(layers, dim - 1, 0))
    return jnp.concatenate(slabs, axis=0)


def empty_layers(field, axis, count):
    shape = list(field.shape)
    shape[axis] = count
    return jnp.zeros(tuple(shape), jnp.float32)


def inbound(full, dim, from_lower, from_upper):
    speeds, weights = lattice()
    axis = dim - 1
    lower_offset = 0
    upper_offset = 0
    layers = []
    for member in range(39):
        field = full[member]
        speed = speeds[member][axis]
        if speed > 0:
            slab = jnp.moveaxis(from_lower[lower_offset : lower_offset + speed], 0, axis)
            lower_offset = lower_offset + speed
            below = jnp.concatenate([empty_layers(field, axis, 3 - speed), slab], axis=axis)
            above = empty_layers(field, axis, 3)
        elif speed < 0:
            slab = jnp.moveaxis(from_upper[upper_offset : upper_offset - speed], 0, axis)
            upper_offset = upper_offset - speed
            below = empty_layers(field, axis, 3)
            above = jnp.concatenate([slab, empty_layers(field, axis, 3 + speed)], axis=axis)
        else:
            below = empty_layers(field, axis, 3)
            above = empty_layers(field, axis, 3)
        layers.append(jnp.concatenate([below, field, above], axis=axis))
    return jnp.stack(layers)


def per_device(populations, relax):
    state = populations
    post = collide(state, relax)
    from_lower = from_behind(outbound(post, 1, 1), "gx", 1)
    from_upper = from_behind(outbound(post, 1, -1), "gx", -1)
    extended = inbound(post, 1, from_lower, from_upper)
    from_lower = from_behind(outbound(extended, 2, 1), "gy", 1)
    from_upper = from_behind(outbound(extended, 2, -1), "gy", -1)
    extended = inbound(extended, 2, from_lower, from_upper)
    from_lower = from_behind(outbound(extended, 3, 1), "gz", 1)
    from_upper = from_behind(outbound(extended, 3, -1), "gz", -1)
    extended = inbound(extended, 3, from_lower, from_upper)
    state = propagate(extended, 3)
    return state


def solution(mesh):
    return jax.shard_map(
        per_device,
        mesh=mesh,
        in_specs=(P(None, "gx", "gy", "gz"), P("gx", "gy", "gz")),
        out_specs=P(None, "gx", "gy", "gz"),
        check_vma=False,
    )
```

profile of v0, /device:TPU:0, one launch (start us, length us, event | category | flops | bytes accessed | tf_op | source)
XLA Modules:
  0.0 99.0 jit_solution(3598783697626491069)
XLA Ops:
  0.0 3.4 %bitcast_subtract_fusion = (f32[8,24,128]{2,1,0:T(8,128)S(1)}, f32[8,24,128]{2,1,0:T(8,128)S(1)}, f32[8,24,128]{2,1,0:T(8,128)S(1)}, f32[8,24,128]{2,1,0:T(8,128...) fusion(f32[8,24,128]{2,1,0:T(8,128)} %param.3, f32[39,8,24,128]{3,2,1,0:T(8,128)} %param.2), kind=kLoop, calls=%fused_computation.549 | loop fusion | flops 7348224 | bytes 4620288 | tf_op jit(solution)/shard_map/sub | solution.py:115
  3.5 1.2 %bitcast_subtract_fusion.4 = (f32[8,24,128]{2,1,0:T(8,128)S(1)}, f32[8,24,128]{2,1,0:T(8,128)S(1)}, f32[8,24,128]{2,1,0:T(8,128)S(1)}, f32[8,24,128]{2,1,0:T(8,1...) fusion(f32[8,24,128]{2,1,0:T(8,128)S(1)} %copy-done.1, ...), kind=kLoop, calls=%fused_computation.572 | loop fusion | flops 9363456 | bytes 3145728 | tf_op jit(solution)/shard_map/sub | solution.py:115
  4.8 1.2 %bitcast_subtract_fusion.12 = (f32[8,24,128]{2,1,0:T(8,128)S(1)}, f32[8,24,128]{2,1,0:T(8,128)S(1)}, f32[8,24,128]{2,1,0:T(8,128)S(1)}, f32[8,24,128]{2,1,0:T(8,...) fusion(f32[8,24,128]{2,1,0:T(8,128)S(1)} %copy-done.1, ...), kind=kLoop, calls=%fused_computation.610 | loop fusion | flops 8945664 | bytes 3047424 | tf_op jit(solution)/shard_map/sub | solution.py:115
  5.9 1.2 %bitcast_subtract_fusion.36 = (f32[8,24,128]{2,1,0:T(8,128)S(1)}, f32[8,24,128]{2,1,0:T(8,128)S(1)}, f32[8,24,128]{2,1,0:T(8,128)S(1)}, f32[8,24,128]{2,1,0:T(8,...) fusion(f32[8,24,128]{2,1,0:T(8,128)S(1)} %copy-done.1, ...), kind=kLoop, calls=%fused_computation.733 | loop fusion | flops 9461760 | bytes 3145728 | tf_op jit(solution)/shard_map/sub | solution.py:115
  7.5 3.0 %collective-permute-start.1 = (f32[18,24,128]{2,1,0:T(8,128)S(1)}, f32[18,24,128]{2,1,0:T(8,128)S(1)}, u32[]{:S(2)}, u32[]{:S(2)}) collective-permute-start(f32[18,24,128]{2,1,0:T(8,128)S(1)} %constant_dynamic-update-slice_fusion.11), channel_id=1, source_target_pairs={{16,0},{0,16},{17,1},{1,17},{18,2},{2,18},{19,3},{3,19},{20,4},{4,... | collective-permute-start | bytes 663560 | tf_op jit(solution)/shard_map/ppermute | solution.py:10
  10.6 0.8 fusion.136
  12.4 0.9 fusion.150
  13.4 0.7 constant_dynamic-update-slice_fusion.60
  14.1 2.7 %collective-permute-done.1 = f32[18,24,128]{2,1,0:T(8,128)S(1)} collective-permute-done((f32[18,24,128]{2,1,0:T(8,128)S(1)}, f32[18,24,128]{2,1,0:T(8,128)S(1)}, u32[]{:S(2)}, u32[]{:S(2)}) %collective-permute-start.1) | collective-permute-done | bytes 221216 | tf_op jit(solution)/shard_map/ppermute | solution.py:10
  17.4 3.2 %collective-permute-done = f32[18,24,128]{2,1,0:T(8,128)S(1)} collective-permute-done((f32[18,24,128]{2,1,0:T(8,128)S(1)}, f32[18,24,128]{2,1,0:T(8,128)S(1)}, u32[]{:S(2)}, u32[]{:S(2)}) %collective-permute-start) | collective-permute-done | bytes 221216 | tf_op jit(solution)/shard_map/ppermute | solution.py:10
  23.8 3.9 %collective-permute-start.3 = (f32[18,14,128]{2,0,1:T(8,128)S(1)}, f32[18,14,128]{2,0,1:T(8,128)}, u32[]{:S(2)}, u32[]{:S(2)}) collective-permute-start(f32[18,14,128]{2,0,1:T(8,128)S(1)} %concatenate.405), channel_id=1, source_target_pairs={{4,0},{8,4},{12,8},{0,12},{5,1},{9,5},{13,9},{1,13},{6,2},{10,6},{... | collective-permute-start | bytes 387080 | tf_op jit(solution)/shard_map/ppermute | solution.py:10
  27.7 2.6 %concatenate.391 = f32[18,14,128]{2,0,1:T(8,128)S(1)} concatenate(f32[1,14,128]{2,0,1:T(1,128)} %get-tuple-element.206, f32[1,14,128]{2,0,1:T(1,128)} %get-tuple-element.191, f32[1,14,128]{2,0,1:T(1,128)} %get-tuple-element.186, f32[1,14,128]{2,0,1:T(1,128)} %get-tuple-element.190, f32[1,14,128]{2,0,1:T(1,128)} %get-tuple-element.187, f32[2,14,128]{2,0,1:T(2,128)S(1)} %get-tuple-element.203, ...), dimensions={0} | concatenate | bytes 258048 | tf_op jit(solution)/shard_map/concatenate | solution.py:150
  30.4 1.4 %fusion.87 = (f32[1,14,30,134]{3,2,1,0:T(8,128)}, f32[1,14,30,134]{3,2,1,0:T(8,128)}) fusion(f32[14,30,3]{2,1,0:T(8,128)S(1)} %broadcast.262, f32[14,3,128]{2,1,0:T(4,128)S(1)} %broadcast.263, f32[1,24,128]{2,1,0:T(8,128)S(1)} %broadcast.303, f32[3,24,128]{2,1,0:T(8,128)S(1)} %broadcast.264, f32[2,24,128]{2,1,0:T(8,128)S(1)} %get-tuple-element.124, ...), kind=kLoop, calls=%fused_computation.347 | loop fusion | flops 787920 | bytes 771696 | tf_op jit(solution)/shard_map/stack | solution.py:182
  31.7 1.0 %fusion.148 = (f32[2,14,30]{0,2,1:T(8,128)}, f32[2,14,30]{0,2,1:T(8,128)}, f32[2,14,30]{0,2,1:T(8,128)}) fusion(f32[14,3,128]{2,1,0:T(4,128)S(1)} %broadcast.263, f32[3,24,128]{2,1,0:T(8,128)S(1)} %broadcast.264, f32[1,24,128]{2,1,0:T(8,128)S(1)} %broadcast.303, f32[2,24,128]{2,1,0:T(8,128)S(1)} %get-tuple-element.125, ...), kind=kLoop, calls=%fused_computation.448 | loop fusion | flops 12600 | bytes 449376 | tf_op jit(solution)/shard_map/transpose | solution.py:149
  32.7 1.8 %slice_bitcast_fusion.34 = (f32[14,1,128]{2,1,0:T(1,128)S(1)}, f32[14,1,128]{2,1,0:T(1,128)S(1)}, f32[14,1,128]{2,1,0:T(1,128)S(1)}, f32[14,1,128]{2,1,0:T(1,128)}, f32[14,1,128]{2,1,0:T(1,128)}) fusion(f32[18,14,128]{2,0,1:T(8,128)} %collective-permute-done.3), kind=kLoop, calls=%fused_computation.1191 | loop fusion | bytes 71680 | tf_op jit(solution)/shard_map/transpose | solution.py:174
  34.6 0.9 fusion.114
  35.5 2.0 %collective-permute-done.2 = f32[18,14,128]{2,0,1:T(8,128)S(1)} collective-permute-done((f32[18,14,128]{2,0,1:T(8,128)S(1)}, f32[18,14,128]{2,0,1:T(8,128)S(1)}, u32[]{:S(2)}, u32[]{:S(2)}) %collective-permute-start.2) | collective-permute-done | bytes 129056 | tf_op jit(solution)/shard_map/ppermute | solution.py:10
  38.2 1.1 %fusion.115 = (f32[1,14,30]{0,2,1:T(8,128)}, f32[1,14,30]{0,2,1:T(8,128)}, f32[1,14,30]{0,2,1:T(8,128)}) fusion(f32[14,2,128]{2,1,0:T(2,128)S(1)} %broadcast.302, f32[2,24,128]{2,1,0:T(8,128)S(1)} %broadcast.288, f32[3,24,128]{2,1,0:T(8,128)S(1)} %broadcast.264, f32[14,3,128]{2,1,0:T(4,128)S(1)} %broadcast.263, f32[14,1,128]{2,1,0:T(1,128)S(1)} %get-tuple-element.154, ...), kind=kLoop, calls=%fused_computation.415 | loop fusion | flops 6720 | bytes 436144 | tf_op jit(solution)/shard_map/transpose | solution.py:149
  39.3 1.0 %fusion.129 = (f32[1,14,30]{0,2,1:T(8,128)}, f32[1,14,30]{0,2,1:T(8,128)}, f32[1,14,30]{0,2,1:T(8,128)}) fusion(f32[14,3,128]{2,1,0:T(4,128)S(1)} %broadcast.263, f32[2,24,128]{2,1,0:T(8,128)S(1)} %broadcast.288, f32[3,24,128]{2,1,0:T(8,128)S(1)} %broadcast.264, f32[14,2,128]{2,1,0:T(2,128)S(1)} %broadcast.302, f32[14,1,128]{2,1,0:T(1,128)S(1)} %get-tuple-element.159, ...), kind=kLoop, calls=%fused_computation.429 | loop fusion | flops 6720 | bytes 436144 | tf_op jit(solution)/shard_map/transpose | solution.py:149
  41.3 1.7 %slice_bitcast_fusion.24 = (f32[14,2,128]{2,1,0:T(2,128)}, f32[14,2,128]{2,1,0:T(2,128)}, f32[14,2,128]{2,1,0:T(2,128)}, f32[14,2,128]{2,1,0:T(2,128)S(1)}, f32[14,2,128]{2,1,0:T(2,128)S(1)}) fusion(f32[18,14,128]{2,0,1:T(8,128)} %collective-permute-done.3), kind=kLoop, calls=%fused_computation.1139 | loop fusion | bytes 143360 | tf_op jit(solution)/shard_map/transpose | solution.py:174
  43.1 0.9 fusion.145
  43.9 2.7 %concatenate.442 = f32[18,14,30]{0,2,1:T(8,128)} concatenate(f32[1,14,30]{0,2,1:T(8,128)} %get-tuple-element.183, f32[1,14,30]{0,2,1:T(8,128)} %get-tuple-element.167, f32[1,14,30]{0,2,1:T(8,128)} %get-tuple-element.168, f32[1,14,30]{0,2,1:T(8,128)} %get-tuple-element.166, f32[1,14,30]{0,2,1:T(8,128)} %get-tuple-element.164, f32[2,14,30]{0,2,1:T(8,128)S(1)} %get-tuple-element.180, ...), dimensions={0} | concatenate | bytes 60480 | tf_op jit(solution)/shard_map/concatenate | solution.py:150
  46.6 1.7 %fusion.108 = (f32[1,14,30]{0,2,1:T(8,128)S(1)}, f32[1,14,30]{0,2,1:T(8,128)}) fusion(f32[14,2,128]{2,1,0:T(2,128)S(1)} %broadcast.302, f32[3,24,128]{2,1,0:T(8,128)S(1)} %broadcast.264, f32[2,24,128]{2,1,0:T(8,128)S(1)} %broadcast.288, f32[14,3,128]{2,1,0:T(4,128)S(1)} %broadcast.263, f32[14,1,128]{2,1,0:T(1,128)} %get-tuple-element.157, ...), kind=kLoop, calls=%fused_computation.408 | loop fusion | flops 5040 | bytes 336160 | tf_op jit(solution)/shard_map/transpose | solution.py:149
  48.4 2.6 %concatenate.424 = f32[18,14,30]{0,2,1:T(8,128)} concatenate(f32[1,14,30]{0,2,1:T(8,128)} %get-tuple-element.184, f32[1,14,30]{0,2,1:T(8,128)} %get-tuple-element.171, f32[1,14,30]{0,2,1:T(8,128)S(1)} %get-tuple-element.170, f32[1,14,30]{0,2,1:T(8,128)} %get-tuple-element.165, f32[1,14,30]{0,2,1:T(8,128)} %get-tuple-element.169, f32[2,14,30]{0,2,1:T(8,128)} %fusion.136, ...), dimensions={0} | concatenate | bytes 60480 | tf_op jit(solution)/shard_map/concatenate | solution.py:150
  51.7 1.5 %fusion.89 = (f32[1,14,30,134]{3,2,1,0:T(8,128)S(1)}, f32[1,14,30,134]{3,2,1,0:T(8,128)S(1)}) fusion(f32[14,30,3]{2,1,0:T(8,128)S(1)} %broadcast.262, f32[14,1,128]{2,1,0:T(1,128)S(1)} %broadcast.305, f32[3,24,128]{2,1,0:T(8,128)S(1)} %broadcast.264, f32[14,3,128]{2,1,0:T(4,128)S(1)} %broadcast.263, f32[14,2,128]{2,1,0:T(2,128)} %get-tuple-element.146, ...), kind=kLoop, calls=%fused_computation.349 | loop fusion | flops 787920 | bytes 746096 | tf_op jit(solution)/shard_map/stack | solution.py:182
  53.2 1.4 %fusion.94 = (f32[1,14,30,134]{3,2,1,0:T(8,128)S(1)}, f32[1,14,30,134]{3,2,1,0:T(8,128)S(1)}) fusion(f32[14,30,3]{2,1,0:T(8,128)S(1)} %broadcast.262, f32[14,1,128]{2,1,0:T(1,128)S(1)} %broadcast.305, f32[1,24,128]{2,1,0:T(8,128)S(1)} %broadcast.303, f32[3,24,128]{2,1,0:T(8,128)S(1)} %broadcast.264, f32[14,3,128]{2,1,0:T(4,128)S(1)} %broadcast.263, ...), kind=kLoop, calls=%fused_computation.354 | loop fusion | flops 900480 | bytes 807536 | tf_op jit(solution)/shard_map/stack | solution.py:182
  54.6 1.4 %fusion.93 = (f32[1,14,30,134]{3,2,1,0:T(8,128)S(1)}, f32[1,14,30,134]{3,2,1,0:T(8,128)S(1)}) fusion(f32[14,30,3]{2,1,0:T(8,128)S(1)} %broadcast.262, f32[14,3,128]{2,1,0:T(4,128)S(1)} %broadcast.263, f32[1,24,128]{2,1,0:T(8,128)S(1)} %broadcast.303, f32[3,24,128]{2,1,0:T(8,128)S(1)} %broadcast.264, f32[14,1,128]{2,1,0:T(1,128)S(1)} %broadcast.305, ...), kind=kLoop, calls=%fused_computation.353 | loop fusion | flops 900480 | bytes 807536 | tf_op jit(solution)/shard_map/stack | solution.py:182
  56.0 0.9 slice_bitcast_fusion.22
  57.4 0.9 slice_bitcast_fusion.23
  59.9 0.7 constant_dynamic-update-slice_fusion.59
  61.7 0.7 constant_dynamic-update-slice_fusion.58
  63.1 0.7 constant_dynamic-update-slice_fusion.57
  64.5 0.7 constant_dynamic-update-slice_fusion.56
  65.9 0.7 constant_dynamic-update-slice_fusion.55
  67.3 0.7 constant_dynamic-update-slice_fusion.54
  68.8 0.7 constant_dynamic-update-slice_fusion.53
  70.3 0.7 constant_dynamic-update-slice_fusion.52
  71.0 0.7 constant_dynamic-update-slice_fusion.51
  71.8 0.7 constant_dynamic-update-slice_fusion.50
  72.5 0.7 constant_dynamic-update-slice_fusion.49
  73.2 0.7 constant_dynamic-update-slice_fusion.48
  74.0 0.7 constant_dynamic-update-slice_fusion.47
  74.7 0.7 constant_dynamic-update-slice_fusion.46
  75.4 1.7 %constant_dynamic-update-slice_fusion.45 = f32[39,8,24,128]{3,2,1,0:T(8,128)} fusion(f32[39,8,24,128]{3,2,1,0:T(8,128)} %constant_dynamic-update-slice_fusion.46, f32[1,14,30,134]{3,2,1,0:T(8,128)} %get-tuple-element.93), kind=kLoop, calls=%fused_computation.533 | loop fusion | bytes 196608
  77.1 1.7 %constant_dynamic-update-slice_fusion.44 = f32[39,8,24,128]{3,2,1,0:T(8,128)} fusion(f32[39,8,24,128]{3,2,1,0:T(8,128)} %constant_dynamic-update-slice_fusion.45, f32[1,14,30,134]{3,2,1,0:T(8,128)} %get-tuple-element.92), kind=kLoop, calls=%fused_computation.532 | loop fusion | bytes 196608
  78.8 0.7 constant_dynamic-update-slice_fusion.43
  79.5 0.7 constant_dynamic-update-slice_fusion.42
  81.7 0.7 constant_dynamic-update-slice_fusion.41
  82.4 0.7 constant_dynamic-update-slice_fusion.40
  83.2 0.7 constant_dynamic-update-slice_fusion.39
  84.6 0.7 constant_dynamic-update-slice_fusion.37
  85.4 0.7 constant_dynamic-update-slice_fusion.36
  86.8 0.7 constant_dynamic-update-slice_fusion.35
  88.1 0.7 constant_dynamic-update-slice_fusion.34
  88.8 0.7 constant_dynamic-update-slice_fusion.33
  89.5 0.7 constant_dynamic-update-slice_fusion.32
  90.3 0.8 fusion.98
  91.0 0.7 constant_dynamic-update-slice_fusion.31
  92.4 0.7 constant_dynamic-update-slice_fusion.30
  93.2 0.7 constant_dynamic-update-slice_fusion.29
  93.9 0.7 constant_dynamic-update-slice_fusion.28
  94.6 0.7 constant_dynamic-update-slice_fusion.27
  95.4 0.7 constant_dynamic-update-slice_fusion.26
  96.8 0.7 constant_dynamic-update-slice_fusion.24
  (243 shorter events, 20.2 us)
Async XLA Ops:
  3.4 9.0 %copy-start.22 = (f32[8,24,128]{2,1,0:T(8,128)}, f32[8,24,128]{2,1,0:T(8,128)S(1)}, u32[]{:S(2)}) copy-start(f32[8,24,128]{2,1,0:T(8,128)S(1)} %get-tuple-element.5) | copy-start | bytes 294916
  4.7 6.8 %copy-start.30 = (f32[8,24,128]{2,1,0:T(8,128)}, f32[8,24,128]{2,1,0:T(8,128)S(1)}, u32[]{:S(2)}) copy-start(f32[8,24,128]{2,1,0:T(8,128)S(1)} %get-tuple-element.64) | copy-start | bytes 294916
  4.7 7.1 %copy-start.8 = (f32[8,24,128]{2,1,0:T(8,128)}, f32[8,24,128]{2,1,0:T(8,128)S(1)}, u32[]{:S(2)}) copy-start(f32[8,24,128]{2,1,0:T(8,128)S(1)} %get-tuple-element.56) | copy-start | bytes 294916
  4.7 7.1 %copy-start.10 = (f32[8,24,128]{2,1,0:T(8,128)}, f32[8,24,128]{2,1,0:T(8,128)S(1)}, u32[]{:S(2)}) copy-start(f32[8,24,128]{2,1,0:T(8,128)S(1)} %get-tuple-element.53) | copy-start | bytes 294916
  4.7 8.6 %copy-start.6 = (f32[8,24,128]{2,1,0:T(8,128)}, f32[8,24,128]{2,1,0:T(8,128)S(1)}, u32[]{:S(2)}) copy-start(f32[8,24,128]{2,1,0:T(8,128)S(1)} %get-tuple-element.54) | copy-start | bytes 294916
  4.7 8.6 %copy-start.7 = (f32[8,24,128]{2,1,0:T(8,128)}, f32[8,24,128]{2,1,0:T(8,128)S(1)}, u32[]{:S(2)}) copy-start(f32[8,24,128]{2,1,0:T(8,128)S(1)} %get-tuple-element.57) | copy-start | bytes 294916
  4.7 16.6 %copy-start.14 = (f32[8,24,128]{2,1,0:T(8,128)}, f32[8,24,128]{2,1,0:T(8,128)S(1)}, u32[]{:S(2)}) copy-start(f32[8,24,128]{2,1,0:T(8,128)S(1)} %get-tuple-element.55) | copy-start | bytes 294916
  4.7 17.2 %copy-start.18 = (f32[8,24,128]{2,1,0:T(8,128)}, f32[8,24,128]{2,1,0:T(8,128)S(1)}, u32[]{:S(2)}) copy-start(f32[8,24,128]{2,1,0:T(8,128)S(1)} %get-tuple-element.58) | copy-start | bytes 294916
  7.2 14.2 %copy-start.4 = (f32[8,24,128]{2,1,0:T(8,128)}, f32[8,24,128]{2,1,0:T(8,128)S(1)}, u32[]{:S(2)}) copy-start(f32[8,24,128]{2,1,0:T(8,128)S(1)} %get-tuple-element.43) | copy-start | bytes 294916
  7.2 15.5 %copy-start.20 = (f32[8,24,128]{2,1,0:T(8,128)}, f32[8,24,128]{2,1,0:T(8,128)S(1)}, u32[]{:S(2)}) copy-start(f32[8,24,128]{2,1,0:T(8,128)S(1)} %get-tuple-element.42) | copy-start | bytes 294916
  7.2 15.5 %copy-start.24 = (f32[8,24,128]{2,1,0:T(8,128)}, f32[8,24,128]{2,1,0:T(8,128)S(1)}, u32[]{:S(2)}) copy-start(f32[8,24,128]{2,1,0:T(8,128)S(1)} %get-tuple-element.49) | copy-start | bytes 294916
  7.2 15.6 %copy-start.26 = (f32[8,24,128]{2,1,0:T(8,128)}, f32[8,24,128]{2,1,0:T(8,128)S(1)}, u32[]{:S(2)}) copy-start(f32[8,24,128]{2,1,0:T(8,128)S(1)} %get-tuple-element.52) | copy-start | bytes 294916
  7.2 16.2 %copy-start.28 = (f32[8,24,128]{2,1,0:T(8,128)}, f32[8,24,128]{2,1,0:T(8,128)S(1)}, u32[]{:S(2)}) copy-start(f32[8,24,128]{2,1,0:T(8,128)S(1)} %get-tuple-element.51) | copy-start | bytes 294916
  7.2 31.0 %copy-start.12 = (f32[8,24,128]{2,1,0:T(8,128)}, f32[8,24,128]{2,1,0:T(8,128)S(1)}, u32[]{:S(2)}) copy-start(f32[8,24,128]{2,1,0:T(8,128)S(1)} %get-tuple-element.41) | copy-start | bytes 294916
  7.2 32.1 %copy-start.16 = (f32[8,24,128]{2,1,0:T(8,128)}, f32[8,24,128]{2,1,0:T(8,128)S(1)}, u32[]{:S(2)}) copy-start(f32[8,24,128]{2,1,0:T(8,128)S(1)} %get-tuple-element.44) | copy-start | bytes 294916
  7.2 33.8 %copy-start.2 = (f32[8,24,128]{2,1,0:T(8,128)}, f32[8,24,128]{2,1,0:T(8,128)S(1)}, u32[]{:S(2)}) copy-start(f32[8,24,128]{2,1,0:T(8,128)S(1)} %get-tuple-element.40) | copy-start | bytes 294916
  7.5 9.3 %collective-permute-start.1 = (f32[18,24,128]{2,1,0:T(8,128)S(1)}, f32[18,24,128]{2,1,0:T(8,128)S(1)}, u32[]{:S(2)}, u32[]{:S(2)}) collective-permute-start(f32[18,24,128]{2,1,0:T(8,128)S(1)} %constant_dynamic-update-slice_fusion.11), channel_id=1, source_target_pairs={{16,0},{0,16},{17,1},{1,17},{18,2},{2,18},{19,3},{3,19},{20,4},{4,... | collective-permute-start | bytes 663560 | tf_op jit(solution)/shard_map/ppermute | solution.py:10
  10.5 10.2 %collective-permute-start = (f32[18,24,128]{2,1,0:T(8,128)S(1)}, f32[18,24,128]{2,1,0:T(8,128)S(1)}, u32[]{:S(2)}, u32[]{:S(2)}) collective-permute-start(f32[18,24,128]{2,1,0:T(8,128)S(1)} %constant_dynamic-update-slice_fusion), channel_id=1, source_target_pairs={{16,0},{0,16},{17,1},{1,17},{18,2},{2,18},{19,3},{3,19},{20,4},{4,... | collective-permute-start | bytes 663560 | tf_op jit(solution)/shard_map/ppermute | solution.py:10
  12.4 15.3 %copy-start.62 = (f32[3,14,128]{2,0,1:T(4,128)S(1)}, f32[3,14,128]{2,0,1:T(4,128)}, u32[]{:S(2)}) copy-start(f32[3,14,128]{2,0,1:T(4,128)} %get-tuple-element.198) | copy-start | bytes 64516
  16.8 6.6 %copy-start.34 = (f32[18,24,128]{2,1,0:T(8,128)}, f32[18,24,128]{2,1,0:T(8,128)S(1)}, u32[]{:S(2)}) copy-start(f32[18,24,128]{2,1,0:T(8,128)S(1)} %collective-permute-done.1) | copy-start | bytes 663556
  17.4 21.9 %copy-start.40 = (f32[1,24,128]{2,1,0:T(8,128)}, f32[1,24,128]{2,1,0:T(8,128)S(1)}, u32[]{:S(2)}) copy-start(f32[1,24,128]{2,1,0:T(8,128)S(1)} %get-tuple-element.134) | copy-start | bytes 36868
  17.4 21.9 %copy-start.42 = (f32[1,24,128]{2,1,0:T(8,128)}, f32[1,24,128]{2,1,0:T(8,128)S(1)}, u32[]{:S(2)}) copy-start(f32[1,24,128]{2,1,0:T(8,128)S(1)} %get-tuple-element.137) | copy-start | bytes 36868
  17.4 21.9 %copy-start.48 = (f32[1,24,128]{2,1,0:T(8,128)}, f32[1,24,128]{2,1,0:T(8,128)S(1)}, u32[]{:S(2)}) copy-start(f32[1,24,128]{2,1,0:T(8,128)S(1)} %get-tuple-element.135) | copy-start | bytes 36868
  17.4 21.9 %copy-start.44 = (f32[1,24,128]{2,1,0:T(8,128)}, f32[1,24,128]{2,1,0:T(8,128)S(1)}, u32[]{:S(2)}) copy-start(f32[1,24,128]{2,1,0:T(8,128)S(1)} %get-tuple-element.136) | copy-start | bytes 36868
  21.3 18.0 %copy-start.50 = (f32[1,24,128]{2,1,0:T(8,128)}, f32[1,24,128]{2,1,0:T(8,128)S(1)}, u32[]{:S(2)}) copy-start(f32[1,24,128]{2,1,0:T(8,128)S(1)} %get-tuple-element.139) | copy-start | bytes 36868
  22.6 18.3 %copy-start.36 = (f32[2,24,128]{2,1,0:T(8,128)}, f32[2,24,128]{2,1,0:T(8,128)S(1)}, u32[]{:S(2)}) copy-start(f32[2,24,128]{2,1,0:T(8,128)S(1)} %get-tuple-element.128) | copy-start | bytes 73732
  22.6 18.3 %copy-start.38 = (f32[2,24,128]{2,1,0:T(8,128)}, f32[2,24,128]{2,1,0:T(8,128)S(1)}, u32[]{:S(2)}) copy-start(f32[2,24,128]{2,1,0:T(8,128)S(1)} %get-tuple-element.127) | copy-start | bytes 73732
  22.7 11.9 %copy-start.39 = (f32[2,24,128]{2,1,0:T(8,128)}, f32[2,24,128]{2,1,0:T(8,128)S(1)}, u32[]{:S(2)}) copy-start(f32[2,24,128]{2,1,0:T(8,128)S(1)} %get-tuple-element.133) | copy-start | bytes 73732
  22.7 18.3 %copy-start.32 = (f32[2,24,128]{2,1,0:T(8,128)}, f32[2,24,128]{2,1,0:T(8,128)S(1)}, u32[]{:S(2)}) copy-start(f32[2,24,128]{2,1,0:T(8,128)S(1)} %get-tuple-element.131) | copy-start | bytes 73732
  22.7 18.6 %copy-start.37 = (f32[2,24,128]{2,1,0:T(8,128)}, f32[2,24,128]{2,1,0:T(8,128)S(1)}, u32[]{:S(2)}) copy-start(f32[2,24,128]{2,1,0:T(8,128)S(1)} %get-tuple-element.132) | copy-start | bytes 73732
  23.8 8.9 %collective-permute-start.3 = (f32[18,14,128]{2,0,1:T(8,128)S(1)}, f32[18,14,128]{2,0,1:T(8,128)}, u32[]{:S(2)}, u32[]{:S(2)}) collective-permute-start(f32[18,14,128]{2,0,1:T(8,128)S(1)} %concatenate.405), channel_id=1, source_target_pairs={{4,0},{8,4},{12,8},{0,12},{5,1},{9,5},{13,9},{1,13},{6,2},{10,6},{... | collective-permute-start | bytes 387080 | tf_op jit(solution)/shard_map/ppermute | solution.py:10
  30.3 7.3 %collective-permute-start.2 = (f32[18,14,128]{2,0,1:T(8,128)S(1)}, f32[18,14,128]{2,0,1:T(8,128)S(1)}, u32[]{:S(2)}, u32[]{:S(2)}) collective-permute-start(f32[18,14,128]{2,0,1:T(8,128)S(1)} %concatenate.391), channel_id=1, source_target_pairs={{12,0},{0,4},{4,8},{8,12},{13,1},{1,5},{5,9},{9,13},{14,2},{2,6},{... | collective-permute-start | bytes 387080 | tf_op jit(solution)/shard_map/ppermute | solution.py:10
  34.6 6.4 %copy-start.69 = (f32[14,1,128]{2,1,0:T(1,128)}, f32[14,1,128]{2,1,0:T(1,128)S(1)}, u32[]{:S(2)}) copy-start(f32[14,1,128]{2,1,0:T(1,128)S(1)} %get-tuple-element.156) | copy-start | bytes 21508
  34.6 6.4 %copy-start.71 = (f32[14,1,128]{2,1,0:T(1,128)}, f32[14,1,128]{2,1,0:T(1,128)S(1)}, u32[]{:S(2)}) copy-start(f32[14,1,128]{2,1,0:T(1,128)S(1)} %get-tuple-element.155) | copy-start | bytes 21508
  34.6 6.4 %copy-start.76 = (f32[14,1,128]{2,1,0:T(1,128)}, f32[14,1,128]{2,1,0:T(1,128)S(1)}, u32[]{:S(2)}) copy-start(f32[14,1,128]{2,1,0:T(1,128)S(1)} %get-tuple-element.154) | copy-start | bytes 21508
  46.6 12.2 %collective-permute-start.5 = (f32[18,14,30]{0,2,1:T(8,128)}, f32[18,14,30]{0,2,1:T(8,128)S(1)}, u32[]{:S(2)}, u32[]{:S(2)}) collective-permute-start(f32[18,14,30]{0,2,1:T(8,128)} %concatenate.442), channel_id=1, source_target_pairs={{1,0},{2,1},{3,2},{0,3},{5,4},{6,5},{7,6},{4,7},{9,8},{10,9},{11,1... | collective-permute-start | bytes 90728 | tf_op jit(solution)/shard_map/ppermute | solution.py:10
  51.0 6.0 %copy-start.11 = (f32[8,24,128]{2,1,0:T(8,128)S(1)}, f32[8,24,128]{2,1,0:T(8,128)}, u32[]{:S(2)}) copy-start(f32[8,24,128]{2,1,0:T(8,128)} %copy-done.10) | copy-start | bytes 294916
  51.0 6.0 %copy-start.27 = (f32[8,24,128]{2,1,0:T(8,128)S(1)}, f32[8,24,128]{2,1,0:T(8,128)}, u32[]{:S(2)}) copy-start(f32[8,24,128]{2,1,0:T(8,128)} %copy-done.26) | copy-start | bytes 294916
  51.0 6.0 %slice-start.1 = ((f32[18,24,128]{2,1,0:T(8,128)}), f32[3,24,128]{2,1,0:T(8,128)S(1)}, s32[]{:S(2)}) async-start(f32[18,24,128]{2,1,0:T(8,128)} %copy-done.35), calls=%async_computation.1 | async-start | bytes 73728 | tf_op jit(solution)/shard_map/slice | solution.py:169
  51.0 7.4 %copy-start.9 = (f32[8,24,128]{2,1,0:T(8,128)S(1)}, f32[8,24,128]{2,1,0:T(8,128)}, u32[]{:S(2)}) copy-start(f32[8,24,128]{2,1,0:T(8,128)} %copy-done.8) | copy-start | bytes 294916
  51.0 7.4 %copy-start.25 = (f32[8,24,128]{2,1,0:T(8,128)S(1)}, f32[8,24,128]{2,1,0:T(8,128)}, u32[]{:S(2)}) copy-start(f32[8,24,128]{2,1,0:T(8,128)} %copy-done.24) | copy-start | bytes 294916
  51.0 7.4 %slice-start = ((f32[18,24,128]{2,1,0:T(8,128)}), f32[3,24,128]{2,1,0:T(8,128)S(1)}, s32[]{:S(2)}) async-start(f32[18,24,128]{2,1,0:T(8,128)} %copy-done.34), calls=%async_computation | async-start | bytes 73728 | tf_op jit(solution)/shard_map/slice | solution.py:174
  51.0 9.7 %collective-permute-start.4 = (f32[18,14,30]{0,2,1:T(8,128)}, f32[18,14,30]{0,2,1:T(8,128)S(1)}, u32[]{:S(2)}, u32[]{:S(2)}) collective-permute-start(f32[18,14,30]{0,2,1:T(8,128)} %concatenate.424), channel_id=1, source_target_pairs={{3,0},{0,1},{1,2},{2,3},{7,4},{4,5},{5,6},{6,7},{11,8},{8,9},{9,10... | collective-permute-start | bytes 90728 | tf_op jit(solution)/shard_map/ppermute | solution.py:10
  54.6 4.6 %copy-start.31 = (f32[8,24,128]{2,1,0:T(8,128)S(1)}, f32[8,24,128]{2,1,0:T(8,128)}, u32[]{:S(2)}) copy-start(f32[8,24,128]{2,1,0:T(8,128)} %copy-done.30) | copy-start | bytes 294916
  54.6 4.6 %copy-start.45 = (f32[1,24,128]{2,1,0:T(8,128)S(1)}, f32[1,24,128]{2,1,0:T(8,128)}, u32[]{:S(2)}) copy-start(f32[1,24,128]{2,1,0:T(8,128)} %copy-done.44) | copy-start | bytes 36868
  54.6 4.6 %copy-start.67 = (f32[14,1,128]{2,1,0:T(1,128)S(1)}, f32[14,1,128]{2,1,0:T(1,128)}, u32[]{:S(2)}) copy-start(f32[14,1,128]{2,1,0:T(1,128)} %copy-done.66) | copy-start | bytes 21508
  54.6 4.6 %copy-start.79 = (f32[1,24,128]{2,1,0:T(8,128)S(1)}, f32[1,24,128]{2,1,0:T(8,128)}, u32[]{:S(2)}) copy-start(f32[1,24,128]{2,1,0:T(8,128)} %get-tuple-element.143) | copy-start | bytes 36868
  60.7 4.5 %copy-start.17 = (f32[8,24,128]{2,1,0:T(8,128)S(1)}, f32[8,24,128]{2,1,0:T(8,128)}, u32[]{:S(2)}) copy-start(f32[8,24,128]{2,1,0:T(8,128)} %copy-done.16) | copy-start | bytes 294916
  60.7 4.5 %copy-start.49 = (f32[1,24,128]{2,1,0:T(8,128)S(1)}, f32[1,24,128]{2,1,0:T(8,128)}, u32[]{:S(2)}) copy-start(f32[1,24,128]{2,1,0:T(8,128)} %copy-done.48) | copy-start | bytes 36868
  60.7 4.5 %copy-start.70 = (f32[14,1,128]{2,1,0:T(1,128)S(1)}, f32[14,1,128]{2,1,0:T(1,128)}, u32[]{:S(2)}) copy-start(f32[14,1,128]{2,1,0:T(1,128)} %copy-done.69) | copy-start | bytes 21508
  61.6 5.0 %copy-start.13 = (f32[8,24,128]{2,1,0:T(8,128)S(1)}, f32[8,24,128]{2,1,0:T(8,128)}, u32[]{:S(2)}) copy-start(f32[8,24,128]{2,1,0:T(8,128)} %copy-done.12) | copy-start | bytes 294916
  61.6 5.0 %copy-start.41 = (f32[1,24,128]{2,1,0:T(8,128)S(1)}, f32[1,24,128]{2,1,0:T(8,128)}, u32[]{:S(2)}) copy-start(f32[1,24,128]{2,1,0:T(8,128)} %copy-done.40) | copy-start | bytes 36868
  61.6 5.0 %copy-start.77 = (f32[14,1,128]{2,1,0:T(1,128)S(1)}, f32[14,1,128]{2,1,0:T(1,128)}, u32[]{:S(2)}) copy-start(f32[14,1,128]{2,1,0:T(1,128)} %copy-done.76) | copy-start | bytes 21508
  63.1 5.0 %copy-start.21 = (f32[8,24,128]{2,1,0:T(8,128)S(1)}, f32[8,24,128]{2,1,0:T(8,128)}, u32[]{:S(2)}) copy-start(f32[8,24,128]{2,1,0:T(8,128)} %copy-done.20) | copy-start | bytes 294916
  63.1 5.0 %copy-start.47 = (f32[1,24,128]{2,1,0:T(8,128)S(1)}, f32[1,24,128]{2,1,0:T(8,128)}, u32[]{:S(2)}) copy-start(f32[1,24,128]{2,1,0:T(8,128)} %copy-done.46) | copy-start | bytes 36868
  63.1 5.0 %copy-start.68 = (f32[14,1,128]{2,1,0:T(1,128)S(1)}, f32[14,1,128]{2,1,0:T(1,128)}, u32[]{:S(2)}) copy-start(f32[14,1,128]{2,1,0:T(1,128)} %get-tuple-element.162) | copy-start | bytes 21508
  65.2 4.4 %copy-start.75 = (f32[14,1,128]{2,1,0:T(1,128)S(1)}, f32[14,1,128]{2,1,0:T(1,128)}, u32[]{:S(2)}) copy-start(f32[14,1,128]{2,1,0:T(1,128)} %copy-done.74) | copy-start | bytes 21508
  70.3 10.8 %copy-start.3 = (f32[8,24,128]{2,1,0:T(8,128)S(1)}, f32[8,24,128]{2,1,0:T(8,128)}, u32[]{:S(2)}) copy-start(f32[8,24,128]{2,1,0:T(8,128)} %copy-done.2) | copy-start | bytes 294916
  70.3 10.8 %copy-start.5 = (f32[8,24,128]{2,1,0:T(8,128)S(1)}, f32[8,24,128]{2,1,0:T(8,128)}, u32[]{:S(2)}) copy-start(f32[8,24,128]{2,1,0:T(8,128)} %copy-done.4) | copy-start | bytes 294916
  80.3 5.8 %copy-start.33 = (f32[2,24,128]{2,1,0:T(8,128)S(1)}, f32[2,24,128]{2,1,0:T(8,128)}, u32[]{:S(2)}) copy-start(f32[2,24,128]{2,1,0:T(8,128)} %copy-done.32) | copy-start | bytes 73732
  81.0 9.2 %copy-start.59 = (f32[14,2,128]{2,1,0:T(2,128)S(1)}, f32[14,2,128]{2,1,0:T(2,128)}, u32[]{:S(2)}) copy-start(f32[14,2,128]{2,1,0:T(2,128)} %copy-done.58) | copy-start | bytes 43012
  81.1 9.2 %copy-start.61 = (f32[14,2,128]{2,1,0:T(2,128)S(1)}, f32[14,2,128]{2,1,0:T(2,128)}, u32[]{:S(2)}) copy-start(f32[14,2,128]{2,1,0:T(2,128)} %copy-done.60) | copy-start | bytes 43012
  85.4 6.4 %copy-start.55 = (f32[14,2,128]{2,1,0:T(2,128)S(1)}, f32[14,2,128]{2,1,0:T(2,128)}, u32[]{:S(2)}) copy-start(f32[14,2,128]{2,1,0:T(2,128)} %copy-done.54) | copy-start | bytes 43012
  85.4 6.4 %copy-start.57 = (f32[14,2,128]{2,1,0:T(2,128)S(1)}, f32[14,2,128]{2,1,0:T(2,128)}, u32[]{:S(2)}) copy-start(f32[14,2,128]{2,1,0:T(2,128)} %copy-done.56) | copy-start | bytes 43012
  (26 other events, 68.8 us)
where the time goes:
time: 100 us; the launch traced here: 99 us
  local copies, waits for them, and re-layouts  48.8 us (49%)
  other arithmetic  33.1 us (33%)
  waiting for transfers between devices  7.9 us (8%)
  starting transfers between devices  7.83 us (8%)
  between operations  1.28 us (1%)
    unnamed x221, local copies, waits for them, and re-layouts  30.2 us
    another operation x20, other arithmetic, inbound(): return jnp.stack(layers)  15 us
    transpose x14, other arithmetic, outbound(): slabs.append(jnp.moveaxis(layers, dim - 1, 0))  11.1 us
    concatenate x6, local copies, waits for them, and re-layouts, outbound(): return jnp.concatenate(slabs, axis=0)  8.28 us
    ppermute x6, waiting for transfers between devices, from_behind(): return lax.ppermute(block, axis, route)  7.9 us
    ppermute x6, starting transfers between devices, from_behind(): return lax.ppermute(block, axis, route)  7.83 us
    sub x4, other arithmetic, collide(): results.append(popul[member] - rate * (popul[member] - maxwellian_target))  7.04 us
    transpose x6, local copies, waits for them, and re-layouts, inbound(): slab = jnp.moveaxis(from_upper[upper_offset:upper_offset - speed], 0, axis)  5.21 us
  transfers between devices with their start and end apart: 6, of which 3 were waited for; matrix products, arithmetic and copies ran while one was open for 25% of the time, Pallas kernels for 0%

commit v1 on v0

v1 whole, which is shorter than its diff:
```python
import functools

import jax
import jax.numpy as jnp
from jax import lax
from jax.experimental import pallas as pl
from jax.experimental.pallas import tpu as pltpu
from jax.sharding import PartitionSpec as P

MESH = pl.DeviceIdType.MESH
AXES = ("gx", "gy", "gz")
PX = 3
PY = 8
GROUP = 32


def lattice():
    speeds = [(0, 0, 0)]
    weights = [1.0 / 12.0]
    for axis in range(3):
        for sign in (1, -1):
            vector = [0, 0, 0]
            vector[axis] = sign
            speeds.append(tuple(vector))
            weights.append(1.0 / 12.0)
    for first in (1, -1):
        for second in (1, -1):
            for third in (1, -1):
                speeds.append((first, second, third))
                weights.append(1.0 / 27.0)
    for axis in range(3):
        for sign in (2, -2):
            vector = [0, 0, 0]
            vector[axis] = sign
            speeds.append(tuple(vector))
            weights.append(2.0 / 135.0)
    for couple in ((0, 1), (0, 2), (1, 2)):
        for first in (2, -2):
            for second in (2, -2):
                vector = [0, 0, 0]
                vector[couple[0]] = first
                vector[couple[1]] = second
                speeds.append(tuple(vector))
                weights.append(1.0 / 432.0)
    for axis in range(3):
        for sign in (3, -3):
            vector = [0, 0, 0]
            vector[axis] = sign
            speeds.append(tuple(vector))
            weights.append(1.0 / 1620.0)
    return (speeds, weights)


SPEEDS, WEIGHTS = lattice()
Q = len(SPEEDS)
SQUARES = [sum(v * v for v in c) for c in SPEEDS]
PAIRS = [
    (m, SPEEDS.index(tuple(-v for v in SPEEDS[m])))
    for m in range(1, Q)
    if m < SPEEDS.index(tuple(-v for v in SPEEDS[m]))
]


def offsets(axis, sign, keep):
    rows, start = [], 0
    for m, c in enumerate(SPEEDS):
        count = c[axis] * sign
        if count > 0 and keep(c):
            rows.append((m, start, count))
            start += count
    return rows


ZCOLS = [offsets(2, sign, lambda c: True) for sign in (1, -1)]
Y1ROWS = [offsets(1, sign, lambda c: c[2] == 0) for sign in (1, -1)]
Y2ROWS = [offsets(1, sign, lambda c: c[2] != 0) for sign in (1, -1)]
Y1SIZE, Y2SIZE = 16, 8

XPURE = [[(SPEEDS.index((s * k, 0, 0)), 1, k) for s in (1, -1)] for k in (1, 2, 3)]
XZ = [(SPEEDS.index((s * 2, 0, 2)), 2, 2) for s in (1, -1)]
XY = [(SPEEDS.index((s * 2, 2, 0)), 2, 2) for s in (1, -1)]
XYZ = [(SPEEDS.index((s, 1, 1)), 4, 1) for s in (1, -1)]


def add_all(terms):
    total = terms[0]
    for term in terms[1:]:
        total = total + term
    return total


def collide(load, rate, emit):
    sums = {k: [] for k in (1, 3, 4, 8, 9)}
    flows = {k: [[], [], []] for k in (1, 3, 4, 8, 9)}
    for m, o in PAIRS:
        up, down = load(m), load(o)
        k = SQUARES[m]
        sums[k].append(up + down)
        diff = up - down
        for axis in range(3):
            if SPEEDS[m][axis] > 0:
                flows[k][axis].append((1, diff))
            elif SPEEDS[m][axis] < 0:
                flows[k][axis].append((-1, diff))
    weight = {SQUARES[m]: WEIGHTS[m] for m in range(Q)}
    size = {1: 1, 3: 1, 4: 2, 8: 2, 9: 3}
    rest = load(0)
    groups = {k: add_all(sums[k]) for k in sums}
    rho = weight[0] * rest
    energy = None
    for k in sums:
        part = weight[k] * groups[k]
        rho = rho + part
        part = part if k == 1 else float(k) * part
        energy = part if energy is None else energy + part
    flux = []
    for axis in range(3):
        total = None
        for k in flows:
            part = None
            for sign, diff in flows[k][axis]:
                if part is None:
                    part = diff if sign > 0 else -diff
                else:
                    part = part + diff if sign > 0 else part - diff
            part = (weight[k] * size[k]) * part
            total = part if total is None else total + part
        flux.append(total)
    inverse = 1.0 / rho
    velocity = [part * inverse for part in flux]
    norm = velocity[0] * velocity[0] + velocity[1] * velocity[1] + velocity[2] * velocity[2]
    t = (energy * inverse - norm) * 0.5 - 1.0
    b = 1.5 * norm
    w = [1.5 * part for part in velocity]
    keep = 1.0 - rate
    k0 = rho * rate
    k24 = k0 * (1.0 / 24.0)
    k6 = k0 * (1.0 / 6.0)
    half_b = 0.5 * b
    kt = k0 * t
    ktb = kt * b
    ktt = kt * t
    base = k0 * (1.0 - half_b + 0.5 * half_b * half_b)
    base1 = k0 * (0.5 - 0.5 * half_b)
    baseo = k0 * (1.0 - half_b)

    def even0(s):
        return (
            base
            + kt * (0.5 * (s - 3.0))
            + ktb * (0.25 * (5.0 - s))
            + ktt * ((s * s - 10.0 * s + 15.0) / 8.0)
        )

    emit(0, keep * rest + even0(0.0))
    for k in sums:
        s = 1.5 * k
        e0 = even0(s)
        e1 = base1 + kt * (0.25 * (s - 7.0))
        o1 = baseo + kt * (0.5 * (s - 5.0))
        for m, o in PAIRS:
            if SQUARES[m] != k:
                continue
            a = None
            for axis in range(3):
                v = SPEEDS[m][axis]
                if v == 0:
                    continue
                unit = w[axis]
                if a is None:
                    a = unit if v > 0 else -unit
                else:
                    a = a + unit if v > 0 else a - unit
            if size[k] != 1:
                a = float(size[k]) * a
            q = a * a
            even = e0 + q * (e1 + q * k24)
            odd = a * (o1 + q * k6)
            emit(m, keep * load(m) + (even + odd))
            emit(o, keep * load(o) + (even - odd))


def kernel(
    pop, rate, ext, g, r, zs, zr, y1s, y1r, y2s, y2r,
    in_sem, z_ss, z_rs, y1_ss, y1_rs, y2_ss, y2_rs, x_ss, x_rs,
):
    nx, ny, nz = pop.shape[1:]
    inner = nx - 4
    groups = [(0, 2), (nx - 2, 2), (2, inner)]
    loads = [
        pltpu.make_async_copy(
            pop.at[:, pl.ds(first, count)], g.at[:, pl.ds(first, count)], in_sem.at[n]
        )
        for n, (first, count) in enumerate(groups)
    ]
    loads.append(pltpu.make_async_copy(rate, r, in_sem.at[3]))
    for n in (3, 0, 1, 2):
        loads[n].start()

    around = []
    for axis in AXES:
        n = lax.axis_size(axis)
        me = lax.axis_index(axis)
        around.append(({axis: lax.rem(me + 1, n)}, {axis: lax.rem(me + n - 1, n)}))
    barrier = pltpu.get_barrier_semaphore()
    for pair in around:
        for target in pair:
            pl.semaphore_signal(barrier, inc=1, device_id=target, device_id_type=MESH)

    lane = lax.broadcasted_iota(jnp.int32, (ny, nz), 1)

    def layer_a(j):
        return j + (j // 2) * (nx - 4)

    def layer_b(j):
        return j + 2

    def rows_at(m):
        start = PY + SPEEDS[m][1]
        return pl.ds(start, ny)

    def edge_rows(sign, count):
        return pl.ds(PY + ny, count) if sign == 0 else pl.ds(PY - count, count)

    def home_rows(sign, count):
        return pl.ds(PY, count) if sign == 0 else pl.ds(PY + ny - count, count)

    def collide_chunk(chunk, layer, steps):
        def step(j, packed):
            x = layer(j)
            packed = list(packed)
            mine = [jnp.zeros((ny, nz), jnp.float32), jnp.zeros((ny, nz), jnp.float32)]
            slot = [{m: (s, c) for m, s, c in ZCOLS[d]} for d in (0, 1)]

            def emit(m, value):
                cx, cy, cz = SPEEDS[m]
                if cz:
                    d = 0 if cz > 0 else 1
                    start, count = slot[d][m]
                    shift = start + count if d == 0 else start
                    moved = pltpu.roll(value, shift, 1) if shift else value
                    mask = (lane >= start) & (lane < start + count)
                    mine[d] = jnp.where(mask, moved, mine[d])
                    value = pltpu.roll(value, cz % nz, 1)
                ext[m, PX + x + cx, rows_at(m), :] = value

            collide(lambda m: g[m, x], r[x], emit)
            for d in (0, 1):
                moved = pltpu.roll(mine[d], GROUP * j, 1)
                mask = (lane >= GROUP * j) & (lane < GROUP * j + GROUP)
                packed[d] = jnp.where(mask, moved, packed[d])
            for d in (0, 1):
                for m, start, count in Y1ROWS[d]:
                    y1s[chunk, d, j, pl.ds(start, count), :] = ext[
                        m, PX + x + SPEEDS[m][0], edge_rows(d, count), :
                    ]
            return tuple(packed)

        blank = jnp.zeros((ny, nz), jnp.float32)
        packed = lax.fori_loop(0, steps, step, (blank, blank))
        for d in (0, 1):
            zs[chunk, d] = packed[d]

    def settle_z(chunk, layer, steps):
        def step(j, carry):
            x = layer(j)
            for d in (0, 1):
                back = lax.rem(nz - GROUP * j, nz)
                base = pltpu.roll(zr[chunk, d], back, 1)
                for m, start, count in ZCOLS[d]:
                    shift = start if d == 0 else start + count
                    moved = pltpu.roll(base, nz - shift, 1) if shift else base
                    mask = lane < count if d == 0 else lane >= nz - count
                    where = (m, PX + x + SPEEDS[m][0], rows_at(m), slice(None))
                    ext[where] = jnp.where(mask, moved, ext[where])
            for d in (0, 1):
                for m, start, count in Y2ROWS[d]:
                    y2s[chunk, d, j, pl.ds(start, count), :] = ext[
                        m, PX + x + SPEEDS[m][0], edge_rows(d, count), :
                    ]
            return carry

        lax.fori_loop(0, steps, step, 0)

    def settle_y(chunk, layer, steps, table, received):
        def step(j, carry):
            x = layer(j)
            for d in (0, 1):
                for m, start, count in table[d]:
                    ext[m, PX + x + SPEEDS[m][0], home_rows(d, count), :] = received[
                        chunk, d, j, pl.ds(start, count), :
                    ]
            return carry

        lax.fori_loop(0, steps, step, 0)

    def send_all(axis, chunk, src, dst, ss, rs):
        copies = []
        for d in (0, 1):
            copies.append(
                pltpu.make_async_remote_copy(
                    src_ref=src.at[chunk, d],
                    dst_ref=dst.at[chunk, d],
                    send_sem=ss.at[chunk, d],
                    recv_sem=rs.at[chunk, d],
                    device_id=around[axis][d],
                    device_id_type=MESH,
                )
            )
        for copy in copies:
            copy.start()
        return copies

    xs = []

    def send_x(pair):
        for d in (0, 1):
            first, members, layers = pair[d]
            n = len(xs)
            out_at = PX + nx if d == 0 else PX - layers
            in_at = PX if d == 0 else PX + nx - layers
            which, rows = pl.ds(first, members), pl.ds(PY, ny)
            copy = pltpu.make_async_remote_copy(
                src_ref=ext.at[which, pl.ds(out_at, layers), rows],
                dst_ref=ext.at[which, pl.ds(in_at, layers), rows],
                send_sem=x_ss.at[n],
                recv_sem=x_rs.at[n],
                device_id=around[0][d],
                device_id_type=MESH,
            )
            copy.start()
            xs.append(copy)

    for n in (3, 0, 1):
        loads[n].wait()
    collide_chunk(0, layer_a, 4)
    pl.semaphore_wait(barrier, 6)
    z_a = send_all(2, 0, zs, zr, z_ss, z_rs)
    y1_a = send_all(1, 0, y1s, y1r, y1_ss, y1_rs)
    send_x(XPURE[0])
    send_x(XPURE[1])
    loads[2].wait()
    collide_chunk(1, layer_b, inner)
    z_b = send_all(2, 1, zs, zr, z_ss, z_rs)
    y1_b = send_all(1, 1, y1s, y1r, y1_ss, y1_rs)
    send_x(XPURE[2])

    for copy in z_a:
        copy.wait_recv()
    settle_z(0, layer_a, 4)
    y2_a = send_all(1, 0, y2s, y2r, y2_ss, y2_rs)
    send_x(XZ)
    for copy in y1_a:
        copy.wait_recv()
    settle_y(0, layer_a, 4, Y1ROWS, y1r)
    send_x(XY)
    for copy in z_b:
        copy.wait_recv()
    settle_z(1, layer_b, inner)
    y2_b = send_all(1, 1, y2s, y2r, y2_ss, y2_rs)
    for copy in y2_a:
        copy.wait_recv()
    settle_y(0, layer_a, 4, Y2ROWS, y2r)
    send_x(XYZ)
    for copy in y1_b:
        copy.wait_recv()
    settle_y(1, layer_b, inner, Y1ROWS, y1r)
    for copy in y2_b:
        copy.wait_recv()
    settle_y(1, layer_b, inner, Y2ROWS, y2r)
    for copy in xs:
        copy.wait_recv()
    for copy in z_a + z_b + y1_a + y1_b + y2_a + y2_b + xs:
        copy.wait_send()


def crop(ext, out, sem):
    nx, ny = out.shape[1:3]
    parts = 3
    share = Q // parts
    copies = [
        pltpu.make_async_copy(
            ext.at[pl.ds(n * share, share), pl.ds(PX, nx), pl.ds(PY, ny)],
            out.at[pl.ds(n * share, share)],
            sem.at[n],
        )
        for n in range(parts)
    ]
    for copy in copies:
        copy.start()
    for copy in copies:
        copy.wait()


def per_device(populations, relax):
    nx, ny, nz = relax.shape
    steps = max(4, nx - 4)
    shape = (Q, nx + 2 * PX, ny + 2 * PY, nz)
    f32 = jnp.float32
    dma = pltpu.SemaphoreType.DMA
    any_space = pl.BlockSpec(memory_space=pl.ANY)
    ext = pl.pallas_call(
        kernel,
        out_shape=pltpu.VMEM(shape, f32),
        in_specs=[any_space, any_space],
        out_specs=pl.BlockSpec(memory_space=pltpu.VMEM),
        scratch_shapes=[
            pltpu.VMEM((Q, nx, ny, nz), f32),
            pltpu.VMEM((nx, ny, nz), f32),
            pltpu.VMEM((2, 2, ny, nz), f32),
            pltpu.VMEM((2, 2, ny, nz), f32),
            pltpu.VMEM((2, 2, steps, Y1SIZE, nz), f32),
            pltpu.VMEM((2, 2, steps, Y1SIZE, nz), f32),
            pltpu.VMEM((2, 2, steps, Y2SIZE, nz), f32),
            pltpu.VMEM((2, 2, steps, Y2SIZE, nz), f32),
            dma((4,)),
            dma((2, 2)), dma((2, 2)),
            dma((2, 2)), dma((2, 2)),
            dma((2, 2)), dma((2, 2)),
            dma((12,)), dma((12,)),
        ],
        compiler_params=pltpu.CompilerParams(
            collective_id=0, has_side_effects=True, vmem_limit_bytes=40 * 2**20
        ),
    )(populations, relax)
    return pl.pallas_call(
        crop,
        out_shape=jax.ShapeDtypeStruct((Q, nx, ny, nz), f32),
        in_specs=[pl.BlockSpec(memory_space=pltpu.VMEM)],
        out_specs=any_space,
        scratch_shapes=[dma((3,))],
    )(ext)


def solution(mesh):
    return jax.shard_map(
        per_device,
        mesh=mesh,
        in_specs=(P(None, "gx", "gy", "gz"), P("gx", "gy", "gz")),
        out_specs=P(None, "gx", "gy", "gz"),
        check_vma=False,
    )
```

time: 100 us -> 29.7 us (0.30)
  local copies, waits for them, and re-layouts: 48.8 us -> 5.12 us
  other arithmetic: 33.1 us -> 0 us
  Pallas kernels: 0 us -> 24.4 us
  waiting for transfers between devices: 7.9 us -> 0 us
  starting transfers between devices: 7.83 us -> 0 us
  between operations: 1.28 us -> 0.02 us
    unnamed x221 -> x4, local copies, waits for them, and re-layouts: 30.2 us -> 5.12 us
    pallas_call x0 -> x2, Pallas kernels: none -> 24.4 us  [the longest x1 18.3 us: per_device(): pl.pallas_call(kernel, out_shape=pltpu.VMEM(shape, f32), in_specs=[any_sp...]
    another operation x20 -> x0, other arithmetic: 15 us -> none  [inbound(): return jnp.stack(layers)]
    transpose x14 -> x0, other arithmetic: 11.1 us -> none  [outbound(): slabs.append(jnp.moveaxis(layers, dim - 1, 0))]
    concatenate x6 -> x0, local copies, waits for them, and re-layouts: 8.28 us -> none  [outbound(): return jnp.concatenate(slabs, axis=0)]
    transpose x12 -> x0, local copies, waits for them, and re-layouts: 8.19 us -> none  [the longest x6 5.21 us: inbound(): slab = jnp.moveaxis(from_upper[upper_offset:upper_offset - speed], 0, axis)]
    ppermute x6 -> x0, waiting for transfers between devices: 7.9 us -> none  [from_behind(): return lax.ppermute(block, axis, route)]
    ppermute x6 -> x0, starting transfers between devices: 7.83 us -> none  [from_behind(): return lax.ppermute(block, axis, route)]
  transfers between devices with their start and end apart: 6 -> 0, of which waited for: 3 -> 0; matrix products, arithmetic and copies ran while one was open for 25% -> 0% of each run, Pallas kernels for 0% -> 0%
where the time goes in v1:
time: 29.7 us; the launch traced here: 29.5 us
  Pallas kernels  24.4 us (82%)
  local copies, waits for them, and re-layouts  5.12 us (17%)
    pallas_call x1, Pallas kernels, per_device(): pl.pallas_call(kernel, out_shape=pltpu.VMEM(shape, f32), in_specs=[any_sp...  18.3 us
    pallas_call x1, Pallas kernels, per_device(): pl.pallas_call(crop, out_shape=jax.ShapeDtypeStruct((Q, nx, ny, nz), f32)...  6.09 us
    unnamed x4, local copies, waits for them, and re-layouts  5.12 us

profile of v1, /device:TPU:0, one launch (start us, length us, event | category | flops | bytes accessed | tf_op | source)
XLA Modules:
  0.0 29.5 jit_solution(1398823192045625831)
XLA Ops:
  0.0 0.0 copy-start.1
  0.0 0.9 %copy-done.1 = f32[8,24,128]{2,1,0:T(8,128)S(1)} copy-done((f32[8,24,128]{2,1,0:T(8,128)S(1)}, f32[8,24,128]{2,1,0:T(8,128)}, u32[]{:S(2)}) %copy-start.1) | copy-done | bytes 98328
  0.9 18.3 %shard_map.28.ext = f32[39,14,40,128]{3,2,1,0:T(8,128)S(1)} custom-call(f32[39,8,24,128]{3,2,1,0:T(8,128)} %pop.1, f32[8,24,128]{2,1,0:T(8,128)S(1)} %copy-done.1), custom_call_target="tpu_custom_call" | custom-call | tf_op jit(solution)/shard_map/pallas_call | solution.py:402
  19.2 0.0 copy-start
  19.2 4.2 %copy-done = f32[39,14,40,128]{3,2,1,0:T(8,128)} copy-done((f32[39,14,40,128]{3,2,1,0:T(8,128)}, f32[39,14,40,128]{3,2,1,0:T(8,128)S(1)}, u32[]{:S(2)}) %copy-start) | copy-done | bytes 11182104
  23.5 6.1 %shard_map.29 = f32[39,8,24,128]{3,2,1,0:T(8,128)} custom-call(f32[39,14,40,128]{3,2,1,0:T(8,128)} %copy-done), custom_call_target="tpu_custom_call" | custom-call | tf_op jit(solution)/shard_map/pallas_call | solution.py:426
Async XLA Ops:
  0.0 0.9 %copy-start.1 = (f32[8,24,128]{2,1,0:T(8,128)S(1)}, f32[8,24,128]{2,1,0:T(8,128)}, u32[]{:S(2)}) copy-start(f32[8,24,128]{2,1,0:T(8,128)} %rate.1) | copy-start | bytes 294916
  19.2 4.2 %copy-start = (f32[39,14,40,128]{3,2,1,0:T(8,128)}, f32[39,14,40,128]{3,2,1,0:T(8,128)S(1)}, u32[]{:S(2)}) copy-start(f32[39,14,40,128]{3,2,1,0:T(8,128)S(1)} %shard_map.28.ext) | copy-start | bytes 33546244

commit v2 on v1

--- a/solution.py
+++ b/solution.py
@@ -1,4 +1,4 @@
-import functools
+import math
 
 import jax
 import jax.numpy as jnp
@@ -399,10 +399,11 @@
     f32 = jnp.float32
     dma = pltpu.SemaphoreType.DMA
     any_space = pl.BlockSpec(memory_space=pl.ANY)
+    room = 67043328 - 4 * math.prod(shape) - 32768
     ext = pl.pallas_call(
         kernel,
         out_shape=pltpu.VMEM(shape, f32),
-        in_specs=[any_space, any_space],
+        in_specs=[pl.BlockSpec(memory_space=pltpu.HBM)] * 2,
         out_specs=pl.BlockSpec(memory_space=pltpu.VMEM),
         scratch_shapes=[
             pltpu.VMEM((Q, nx, ny, nz), f32),
@@ -420,15 +421,16 @@
             dma((12,)), dma((12,)),
         ],
         compiler_params=pltpu.CompilerParams(
-            collective_id=0, has_side_effects=True, vmem_limit_bytes=40 * 2**20
+            collective_id=0, has_side_effects=True, vmem_limit_bytes=room
         ),
     )(populations, relax)
     return pl.pallas_call(
         crop,
         out_shape=jax.ShapeDtypeStruct((Q, nx, ny, nz), f32),
-        in_specs=[pl.BlockSpec(memory_space=pltpu.VMEM)],
+        in_specs=[any_space],
         out_specs=any_space,
         scratch_shapes=[dma((3,))],
+        compiler_params=pltpu.CompilerParams(vmem_limit_bytes=2**20),
     )(ext)
 
 

time: 29.7 us -> 20.4 us (0.69)
  local copies, waits for them, and re-layouts: 5.12 us -> 0 us
  Pallas kernels: 24.4 us -> 20.2 us
    unnamed x4 -> x0, local copies, waits for them, and re-layouts: 5.12 us -> none
    pallas_call x1, Pallas kernels: 6.09 us -> 1.92 us  [per_device(): pl.pallas_call(crop, out_shape=jax.ShapeDtypeStruct((Q, nx, ny, nz), f32)...]
where the time goes in v2:
time: 20.4 us; the launch traced here: 20.2 us
  Pallas kernels  20.2 us (99%)
    pallas_call x1, Pallas kernels, per_device(): pl.pallas_call(kernel, out_shape=pltpu.VMEM(shape, f32), in_specs=[pl.Blo...  18.3 us
    pallas_call x1, Pallas kernels, per_device(): pl.pallas_call(crop, out_shape=jax.ShapeDtypeStruct((Q, nx, ny, nz), f32)...  1.92 us

profile of v2, /device:TPU:0, one launch (start us, length us, event | category | flops | bytes accessed | tf_op | source)
XLA Modules:
  0.0 20.2 jit_solution(1032441908573458453)
XLA Ops:
  0.0 18.3 %shard_map.28.ext = f32[39,14,40,128]{3,2,1,0:T(8,128)S(1)} custom-call(f32[39,8,24,128]{3,2,1,0:T(8,128)} %pop.1, f32[8,24,128]{2,1,0:T(8,128)} %rate.1), custom_call_target="tpu_custom_call" | custom-call | tf_op jit(solution)/shard_map/pallas_call | solution.py:403
  18.3 1.9 %shard_map.29 = f32[39,8,24,128]{3,2,1,0:T(8,128)} custom-call(f32[39,14,40,128]{3,2,1,0:T(8,128)S(1)} %shard_map.28.ext), custom_call_target="tpu_custom_call" | custom-call | tf_op jit(solution)/shard_map/pallas_call | solution.py:427

commit v3 on v2

--- a/solution.py
+++ b/solution.py
@@ -78,8 +78,8 @@
 
 XPURE = [[(SPEEDS.index((s * k, 0, 0)), 1, k) for s in (1, -1)] for k in (1, 2, 3)]
 XZ = [(SPEEDS.index((s * 2, 0, 2)), 2, 2) for s in (1, -1)]
-XY = [(SPEEDS.index((s * 2, 2, 0)), 2, 2) for s in (1, -1)]
-XYZ = [(SPEEDS.index((s, 1, 1)), 4, 1) for s in (1, -1)]
+XY = [[(SPEEDS.index((s * 2, k, 0)), 1, 2) for s in (1, -1)] for k in (2, -2)]
+XYZ = [[(SPEEDS.index((s, k, 1)), 2, 1) for s in (1, -1)] for k in (1, -1)]
 
 
 def add_all(terms):
@@ -312,14 +312,17 @@
         return copies
 
     xs = []
-
-    def send_x(pair):
+    early = [(8, ny - 8), (0, ny - 8)]
+    late = [(0, 8), (ny - 8, 8)]
+
+    def send_x(pair, rows=None):
+        start, count = rows or (0, ny)
         for d in (0, 1):
             first, members, layers = pair[d]
             n = len(xs)
             out_at = PX + nx if d == 0 else PX - layers
             in_at = PX if d == 0 else PX + nx - layers
-            which, rows = pl.ds(first, members), pl.ds(PY, ny)
+            which, rows = pl.ds(first, members), pl.ds(PY + start, count)
             copy = pltpu.make_async_remote_copy(
                 src_ref=ext.at[which, pl.ds(out_at, layers), rows],
                 dst_ref=ext.at[which, pl.ds(in_at, layers), rows],
@@ -339,6 +342,8 @@
     y1_a = send_all(1, 0, y1s, y1r, y1_ss, y1_rs)
     send_x(XPURE[0])
     send_x(XPURE[1])
+    for n in (0, 1):
+        send_x(XY[n], early[n])
     loads[2].wait()
     collide_chunk(1, layer_b, inner)
     z_b = send_all(2, 1, zs, zr, z_ss, z_rs)
@@ -350,10 +355,13 @@
     settle_z(0, layer_a, 4)
     y2_a = send_all(1, 0, y2s, y2r, y2_ss, y2_rs)
     send_x(XZ)
+    for n in (0, 1):
+        send_x(XYZ[n], early[n])
     for copy in y1_a:
         copy.wait_recv()
     settle_y(0, layer_a, 4, Y1ROWS, y1r)
-    send_x(XY)
+    for n in (0, 1):
+        send_x(XY[n], late[n])
     for copy in z_b:
         copy.wait_recv()
     settle_z(1, layer_b, inner)
@@ -361,7 +369,8 @@
     for copy in y2_a:
         copy.wait_recv()
     settle_y(0, layer_a, 4, Y2ROWS, y2r)
-    send_x(XYZ)
+    for n in (0, 1):
+        send_x(XYZ[n], late[n])
     for copy in y1_b:
         copy.wait_recv()
     settle_y(1, layer_b, inner, Y1ROWS, y1r)
@@ -418,7 +427,7 @@
             dma((2, 2)), dma((2, 2)),
             dma((2, 2)), dma((2, 2)),
             dma((2, 2)), dma((2, 2)),
-            dma((12,)), dma((12,)),
+            dma((24,)), dma((24,)),
         ],
         compiler_params=pltpu.CompilerParams(
             collective_id=0, has_side_effects=True, vmem_limit_bytes=room

time: 20.4 us -> 19.5 us (0.956)
  Pallas kernels: 20.2 us -> 19.3 us
    pallas_call x1, Pallas kernels: 18.3 us -> 17.4 us  [per_device(): pl.pallas_call(kernel, out_shape=pltpu.VMEM(shape, f32), in_specs=[pl.Blo...]
where the time goes in v3:
time: 19.5 us; the launch traced here: 19.3 us
  Pallas kernels  19.3 us (99%)
    pallas_call x1, Pallas kernels, per_device(): pl.pallas_call(kernel, out_shape=pltpu.VMEM(shape, f32), in_specs=[pl.Blo...  17.4 us
    pallas_call x1, Pallas kernels, per_device(): pl.pallas_call(crop, out_shape=jax.ShapeDtypeStruct((Q, nx, ny, nz), f32)...  1.92 us

profile of v3, /device:TPU:0, one launch (start us, length us, event | category | flops | bytes accessed | tf_op | source)
XLA Modules:
  0.0 19.3 jit_solution(4222681063177733697)
XLA Ops:
  0.0 17.4 %shard_map.28.ext = f32[39,14,40,128]{3,2,1,0:T(8,128)S(1)} custom-call(f32[39,8,24,128]{3,2,1,0:T(8,128)} %pop.1, f32[8,24,128]{2,1,0:T(8,128)} %rate.1), custom_call_target="tpu_custom_call" | custom-call | tf_op jit(solution)/shard_map/pallas_call | solution.py:412
  17.4 1.9 %shard_map.29 = f32[39,8,24,128]{3,2,1,0:T(8,128)} custom-call(f32[39,14,40,128]{3,2,1,0:T(8,128)S(1)} %shard_map.28.ext), custom_call_target="tpu_custom_call" | custom-call | tf_op jit(solution)/shard_map/pallas_call | solution.py:436

commit v4 on v3

--- a/solution.py
+++ b/solution.py
@@ -182,7 +182,7 @@
 
 def kernel(
     pop, rate, ext, g, r, zs, zr, y1s, y1r, y2s, y2r,
-    in_sem, z_ss, z_rs, y1_ss, y1_rs, y2_ss, y2_rs, x_ss, x_rs,
+    in_sem, z_ss, z_rs, y1_ss, y1_rs, y2_ss, y2_rs, x_ss, x_rs, token,
 ):
     nx, ny, nz = pop.shape[1:]
     inner = nx - 4
@@ -203,9 +203,41 @@
         me = lax.axis_index(axis)
         around.append(({axis: lax.rem(me + 1, n)}, {axis: lax.rem(me + n - 1, n)}))
     barrier = pltpu.get_barrier_semaphore()
-    for pair in around:
-        for target in pair:
+    for axis in (0, 2):
+        for target in around[axis]:
             pl.semaphore_signal(barrier, inc=1, device_id=target, device_id_type=MESH)
+    long = lax.axis_size("gy")
+    row = lax.axis_index("gy")
+    relayed = long > 2
+    ends = (long - 1, 0)
+    for d in (0, 1):
+        if relayed:
+            @pl.when(row != ends[d])
+            def _():
+                pl.semaphore_signal(barrier, inc=1, device_id=around[1][d], device_id_type=MESH)
+        else:
+            pl.semaphore_signal(barrier, inc=1, device_id=around[1][d], device_id_type=MESH)
+
+    def relay(d):
+        @pl.when(row != ends[1 - d])
+        def _():
+            pl.semaphore_wait(token.at[d], 1)
+
+        @pl.when(row != ends[d])
+        def _():
+            pl.semaphore_signal(token.at[d], inc=1, device_id=around[1][d], device_id_type=MESH)
+
+    def relay_near(first):
+        if not relayed:
+            return
+
+        @pl.when(row < long // 2 if first else row >= long // 2)
+        def _():
+            relay(0)
+
+        @pl.when(row >= long // 2 if first else row < long // 2)
+        def _():
+            relay(1)
 
     lane = lax.broadcasted_iota(jnp.int32, (ny, nz), 1)
 
@@ -294,7 +326,7 @@
 
         lax.fori_loop(0, steps, step, 0)
 
-    def send_all(axis, chunk, src, dst, ss, rs):
+    def send_all(axis, chunk, src, dst, ss, rs, start=True):
         copies = []
         for d in (0, 1):
             copies.append(
@@ -307,9 +339,21 @@
                     device_id_type=MESH,
                 )
             )
-        for copy in copies:
-            copy.start()
+        if start:
+            for copy in copies:
+                copy.start()
         return copies
+
+    def start_y(copies, wrap):
+        for d in (0, 1):
+            if not relayed:
+                if not wrap:
+                    copies[d].start()
+                continue
+
+            @pl.when(row == ends[d] if wrap else row != ends[d])
+            def _():
+                copies[d].start()
 
     xs = []
     early = [(8, ny - 8), (0, ny - 8)]
@@ -337,15 +381,30 @@
     for n in (3, 0, 1):
         loads[n].wait()
     collide_chunk(0, layer_a, 4)
-    pl.semaphore_wait(barrier, 6)
+    if relayed:
+        at_end = (row == 0) | (row == long - 1)
+
+        @pl.when(at_end)
+        def _():
+            pl.semaphore_wait(barrier, 5)
+
+        @pl.when(jnp.logical_not(at_end))
+        def _():
+            pl.semaphore_wait(barrier, 6)
+    else:
+        pl.semaphore_wait(barrier, 6)
     z_a = send_all(2, 0, zs, zr, z_ss, z_rs)
-    y1_a = send_all(1, 0, y1s, y1r, y1_ss, y1_rs)
+    y1_a = send_all(1, 0, y1s, y1r, y1_ss, y1_rs, start=False)
+    start_y(y1_a, False)
     send_x(XPURE[0])
     send_x(XPURE[1])
     for n in (0, 1):
         send_x(XY[n], early[n])
     loads[2].wait()
+    relay_near(True)
     collide_chunk(1, layer_b, inner)
+    relay_near(False)
+    start_y(y1_a, True)
     z_b = send_all(2, 1, zs, zr, z_ss, z_rs)
     y1_b = send_all(1, 1, y1s, y1r, y1_ss, y1_rs)
     send_x(XPURE[2])
@@ -428,6 +487,7 @@
             dma((2, 2)), dma((2, 2)),
             dma((2, 2)), dma((2, 2)),
             dma((24,)), dma((24,)),
+            pltpu.SemaphoreType.REGULAR((2,)),
         ],
         compiler_params=pltpu.CompilerParams(
             collective_id=0, has_side_effects=True, vmem_limit_bytes=room

time: 19.5 us -> 21.2 us (1.087)
  Pallas kernels: 19.3 us -> 21.1 us
    pallas_call x1, Pallas kernels: 17.4 us -> 19.2 us  [per_device(): pl.pallas_call(kernel, out_shape=pltpu.VMEM(shape, f32), in_specs=[pl.Blo...]
where the time goes in v4:
time: 21.2 us; the launch traced here: 21.1 us
  Pallas kernels  21.1 us (100%)
    pallas_call x1, Pallas kernels, per_device(): pl.pallas_call(kernel, out_shape=pltpu.VMEM(shape, f32), in_specs=[pl.Blo...  19.2 us
    pallas_call x1, Pallas kernels, per_device(): pl.pallas_call(crop, out_shape=jax.ShapeDtypeStruct((Q, nx, ny, nz), f32)...  1.92 us

profile of v4, /device:TPU:0, one launch (start us, length us, event | category | flops | bytes accessed | tf_op | source)
XLA Modules:
  0.0 21.1 jit_solution(16210569787501668601)
XLA Ops:
  0.0 19.2 %shard_map.28.ext = f32[39,14,40,128]{3,2,1,0:T(8,128)S(1)} custom-call(f32[39,8,24,128]{3,2,1,0:T(8,128)} %pop.1, f32[8,24,128]{2,1,0:T(8,128)} %rate.1), custom_call_target="tpu_custom_call" | custom-call | tf_op jit(solution)/shard_map/pallas_call | solution.py:471
  19.2 1.9 %shard_map.29 = f32[39,8,24,128]{3,2,1,0:T(8,128)} custom-call(f32[39,14,40,128]{3,2,1,0:T(8,128)S(1)} %shard_map.28.ext), custom_call_target="tpu_custom_call" | custom-call | tf_op jit(solution)/shard_map/pallas_call | solution.py:496

commit v5 on v3

--- a/solution.py
+++ b/solution.py
@@ -186,16 +186,14 @@
 ):
     nx, ny, nz = pop.shape[1:]
     inner = nx - 4
-    groups = [(0, 2), (nx - 2, 2), (2, inner)]
+    groups = [(0, 1), (nx - 1, 1), (1, 1), (nx - 2, 1), (2, inner)]
     loads = [
         pltpu.make_async_copy(
             pop.at[:, pl.ds(first, count)], g.at[:, pl.ds(first, count)], in_sem.at[n]
         )
         for n, (first, count) in enumerate(groups)
     ]
-    loads.append(pltpu.make_async_copy(rate, r, in_sem.at[3]))
-    for n in (3, 0, 1, 2):
-        loads[n].start()
+    loads.append(pltpu.make_async_copy(rate, r, in_sem.at[5]))
 
     around = []
     for axis in AXES:
@@ -203,14 +201,16 @@
         me = lax.axis_index(axis)
         around.append(({axis: lax.rem(me + 1, n)}, {axis: lax.rem(me + n - 1, n)}))
     barrier = pltpu.get_barrier_semaphore()
-    for pair in around:
+    for pair in (around[1], around[0], around[2]):
         for target in pair:
             pl.semaphore_signal(barrier, inc=1, device_id=target, device_id_type=MESH)
+    for n in (5, 0, 1, 2, 3, 4):
+        loads[n].start()
 
     lane = lax.broadcasted_iota(jnp.int32, (ny, nz), 1)
 
     def layer_a(j):
-        return j + (j // 2) * (nx - 4)
+        return (j % 2) * (nx - 1) + (j // 2) * (1 - 2 * (j % 2))
 
     def layer_b(j):
         return j + 2
@@ -225,7 +225,7 @@
     def home_rows(sign, count):
         return pl.ds(PY, count) if sign == 0 else pl.ds(PY + ny - count, count)
 
-    def collide_chunk(chunk, layer, steps):
+    def collide_chunk(chunk, layer, first, last, packed=None):
         def step(j, packed):
             x = layer(j)
             packed = list(packed)
@@ -257,7 +257,9 @@
             return tuple(packed)
 
         blank = jnp.zeros((ny, nz), jnp.float32)
-        packed = lax.fori_loop(0, steps, step, (blank, blank))
+        return lax.fori_loop(first, last, step, packed or (blank, blank))
+
+    def pack_z(chunk, packed):
         for d in (0, 1):
             zs[chunk, d] = packed[d]
 
@@ -334,18 +336,21 @@
             copy.start()
             xs.append(copy)
 
-    for n in (3, 0, 1):
+    for n in (5, 0, 1):
         loads[n].wait()
-    collide_chunk(0, layer_a, 4)
+    packed = collide_chunk(0, layer_a, 0, 2)
+    loads[2].wait()
+    loads[3].wait()
+    pack_z(0, collide_chunk(0, layer_a, 2, 4, packed))
     pl.semaphore_wait(barrier, 6)
+    send_x(XPURE[0])
+    send_x(XPURE[1])
     z_a = send_all(2, 0, zs, zr, z_ss, z_rs)
     y1_a = send_all(1, 0, y1s, y1r, y1_ss, y1_rs)
-    send_x(XPURE[0])
-    send_x(XPURE[1])
     for n in (0, 1):
         send_x(XY[n], early[n])
-    loads[2].wait()
-    collide_chunk(1, layer_b, inner)
+    loads[4].wait()
+    pack_z(1, collide_chunk(1, layer_b, 0, inner))
     z_b = send_all(2, 1, zs, zr, z_ss, z_rs)
     y1_b = send_all(1, 1, y1s, y1r, y1_ss, y1_rs)
     send_x(XPURE[2])
@@ -423,7 +428,7 @@
             pltpu.VMEM((2, 2, steps, Y1SIZE, nz), f32),
             pltpu.VMEM((2, 2, steps, Y2SIZE, nz), f32),
             pltpu.VMEM((2, 2, steps, Y2SIZE, nz), f32),
-            dma((4,)),
+            dma((6,)),
             dma((2, 2)), dma((2, 2)),
             dma((2, 2)), dma((2, 2)),
             dma((2, 2)), dma((2, 2)),

time: 19.5 us -> 19.3 us (0.990)
  Pallas kernels: 19.3 us -> 19.1 us
where the time goes in v5:
time: 19.3 us; the launch traced here: 19.1 us
  Pallas kernels  19.1 us (99%)
    pallas_call x1, Pallas kernels, per_device(): pl.pallas_call(kernel, out_shape=pltpu.VMEM(shape, f32), in_specs=[pl.Blo...  17.2 us
    pallas_call x1, Pallas kernels, per_device(): pl.pallas_call(crop, out_shape=jax.ShapeDtypeStruct((Q, nx, ny, nz), f32)...  1.92 us

profile of v5, /device:TPU:0, one launch (start us, length us, event | category | flops | bytes accessed | tf_op | source)
XLA Modules:
  0.0 19.1 jit_solution(8244309094314109296)
XLA Ops:
  0.0 17.2 %shard_map.28.ext = f32[39,14,40,128]{3,2,1,0:T(8,128)S(1)} custom-call(f32[39,8,24,128]{3,2,1,0:T(8,128)} %pop.1, f32[8,24,128]{2,1,0:T(8,128)} %rate.1), custom_call_target="tpu_custom_call" | custom-call | tf_op jit(solution)/shard_map/pallas_call | solution.py:417
  17.2 1.9 %shard_map.29 = f32[39,8,24,128]{3,2,1,0:T(8,128)} custom-call(f32[39,14,40,128]{3,2,1,0:T(8,128)S(1)} %shard_map.28.ext), custom_call_target="tpu_custom_call" | custom-call | tf_op jit(solution)/shard_map/pallas_call | solution.py:441
